TPU v7x, 32 devices: a whole 2x2x4 slice. The times are simulated.
32 devices in a mesh: groups: 2 (over y), rows: 16 (over z, x, core).
Axes of the slice: x: 2, y: 2, z: 4, core: 2. Of those that a mesh axis runs over, the one named last changes fastest.
Arguments:
- pair_repr: bfloat16 [256, 128, 128], P('groups', 'rows'), parts along dimension 0, may hold values from -6 to 6
- single_repr: bfloat16 [256, 384], P(('groups', 'rows')), parts along dimension 0, may hold values from -6 to 6
- residue_index: int32 [256], P('groups'), parts along dimension 0, may hold values from 0 to 47
- chain_index: int32 [256], P('groups'), parts along dimension 0, may hold values from 0 to 3
- complex_index: int32 [256], P('groups'), parts along dimension 0, may hold values from 0 to 7, never falling along the last dimension, each value on 1 to 96 neighbouring positions
- pad_mask: int32 [256], P('groups'), parts along dimension 0, may hold values 0 or 1
- w_query: bfloat16 [384, 384], replicated, may hold values from -3 to 3
- w_key: bfloat16 [384, 384], replicated, may hold values from -3.1 to 3.1
- w_value: bfloat16 [384, 384], replicated, may hold values from -0.3125 to 0.3125
- w_gate: bfloat16 [384, 384], replicated, may hold values from -0.3125 to 0.3125
- w_out: bfloat16 [384, 384], replicated, may hold values from -2.5 to 2.5
- w_bias: bfloat16 [128, 16], replicated, may hold values from -0.5 to 0.5
- rel_table: bfloat16 [66, 128], replicated, may hold values from -6 to 6
- w_mix_a: bfloat16 [384, 128], replicated, may hold values from -0.3125 to 0.3125
- w_mix_b: bfloat16 [384, 128], replicated, may hold values from -0.3125 to 0.3125
- w_hidden_a: bfloat16 [128, 512], replicated, may hold values from -0.5 to 0.5
- w_hidden_b: bfloat16 [128, 512], replicated, may hold values from -0.5 to 0.5
- w_hidden_out: bfloat16 [512, 128], replicated, may hold values from -0.25 to 0.25
- w_pae: bfloat16 [128, 64], replicated, may hold values from -30 to 30
- pae_bias: float32 [64], replicated, may hold values from -4 to 4
Outputs:
- refined: bfloat16 [256, 384], P(('groups', 'rows')), parts along dimension 0
- errors: float32 [256, 128], P(('groups', 'rows')), parts along dimension 0
There are 2 independent parts, one for each index of `groups`. A program takes and returns all parts, laid end to end along the dimension named above; an argument that names none is the same for every part. Nothing has to cross between parts.
Inputs may be any that keep to these rules, and one draw needn't show every extreme that they name: `complex_index`: never falls along the tokens; each complex holds 1 to 96 consecutive tokens.
All inputs are finite; a program needn't handle non-finite values.
Results may differ from a plain program's by a relative error of at most 0.023.
Values may be sent and summed in bfloat16 or wider, within the bound.
A program may use at most 128 MiB of HBM per device.

v0:
```python
import math

import jax
import jax.numpy as jnp
from jax import lax
from jax.sharding import PartitionSpec as P

epsilon = 1e-05
masked_score = -1e30


def norm_rows(values):
    center = values - jnp.mean(values, axis=-1, keepdims=True)
    spread = jnp.mean(center * center, axis=-1, keepdims=True)
    return center * lax.rsqrt(spread + epsilon)


def relative(res_query, chain_query, res_key, chain_key, rel_table):
    reach = (rel_table.shape[0] - 2) // 2
    offsets = jnp.clip(res_query[:, None] - res_key[None, :], -reach, reach) + reach
    bucket = jnp.where(chain_query[:, None] == chain_key[None, :], offsets, 2 * reach + 1)
    classes = jnp.arange(rel_table.shape[0], dtype=jnp.int32)
    onehot = (bucket[:, :, None] == classes[None, None, :]).astype(jnp.bfloat16)
    return jnp.einsum("qkr,rc->qkc", onehot, rel_table, preferred_element_type=jnp.float32)


def pair_tail(mixed, w_hidden_a, w_hidden_b, w_hidden_out, w_pae, pae_bias):
    width = mixed.shape[-1]
    flat = mixed.reshape(-1, width)
    normed = norm_rows(flat).astype(jnp.bfloat16)
    gate_part = jnp.dot(normed, w_hidden_a, preferred_element_type=jnp.float32)
    up_part = jnp.dot(normed, w_hidden_b, preferred_element_type=jnp.float32)
    hidden = (jax.nn.silu(gate_part) * up_part).astype(jnp.bfloat16)
    updated = flat + jnp.dot(hidden, w_hidden_out, preferred_element_type=jnp.float32)
    final = norm_rows(updated).astype(jnp.bfloat16)
    logits = jnp.dot(final, w_pae, preferred_element_type=jnp.float32) + pae_bias[None, :]
    probs = jax.nn.softmax(logits, axis=-1)
    bins = w_pae.shape[1]
    centers = (jnp.arange(bins, dtype=jnp.float32) + 0.5) * (32.0 / bins)
    return jnp.sum(probs * centers[None, :], axis=-1).reshape(mixed.shape[:-1])


def on_device(
    pair_repr,
    single_repr,
    residue_index,
    chain_index,
    complex_index,
    pad_mask,
    w_query,
    w_key,
    w_value,
    w_gate,
    w_out,
    w_bias,
    rel_table,
    w_mix_a,
    w_mix_b,
    w_hidden_a,
    w_hidden_b,
    w_hidden_out,
    w_pae,
    pae_bias,
):
    local_rows = single_repr.shape[0]
    head_count = w_bias.shape[1]
    head_size = single_repr.shape[1] // head_count
    first_row = lax.axis_index("rows") * local_rows
    row_ids = first_row + jnp.arange(local_rows, dtype=jnp.int32)
    res_local = lax.dynamic_slice_in_dim(residue_index, first_row, local_rows, 0)
    chain_local = lax.dynamic_slice_in_dim(chain_index, first_row, local_rows, 0)
    complex_local = lax.dynamic_slice_in_dim(complex_index, first_row, local_rows, 0)
    normed = norm_rows(single_repr.astype(jnp.float32)).astype(jnp.bfloat16)
    queries = jnp.dot(normed, w_query, preferred_element_type=jnp.float32).astype(jnp.bfloat16)
    keys_local = jnp.dot(normed, w_key, preferred_element_type=jnp.float32).astype(jnp.bfloat16)
    values_local = jnp.dot(normed, w_value, preferred_element_type=jnp.float32).astype(jnp.bfloat16)
    gating = jax.nn.sigmoid(jnp.dot(normed, w_gate, preferred_element_type=jnp.float32))
    pair_local = lax.all_to_all(pair_repr, "rows", split_axis=0, concat_axis=1, tiled=True)
    pair_in = pair_local.astype(jnp.float32) + relative(
        res_local, chain_local, residue_index, chain_index, rel_table
    )
    pair_bias = jnp.einsum(
        "qkc,ch->hqk",
        norm_rows(pair_in).astype(jnp.bfloat16),
        w_bias,
        preferred_element_type=jnp.float32,
    ).astype(jnp.bfloat16)
    query_heads = queries.reshape(local_rows, head_count, head_size)
    row_max = jnp.full((head_count, local_rows), masked_score, jnp.float32)
    key_part = lax.all_gather(keys_local, "rows", axis=0, tiled=True)
    value_part = lax.all_gather(values_local, "rows", axis=0, tiled=True)
    count = key_part.shape[0]
    key_heads = key_part.reshape(count, head_count, head_size)
    value_heads = value_part.reshape(count, head_count, head_size)
    scores = jnp.einsum(
        "qhd,khd->hqk", query_heads, key_heads, preferred_element_type=jnp.float32
    ) / math.sqrt(head_size)
    scores = scores + pair_bias.astype(jnp.float32)
    key_ids = jnp.arange(count, dtype=jnp.int32)
    allowed = (complex_local[:, None] == complex_index[None, :]) & (
        (pad_mask[None, :] == 1) | (row_ids[:, None] == key_ids[None, :])
    )
    scores = jnp.where(allowed[None], scores, masked_score)
    new_max = jnp.maximum(row_max, jnp.max(scores, axis=-1))
    expo = jnp.exp(scores - new_max[..., None])
    new_sum = jnp.sum(expo, axis=-1)
    added = jnp.einsum(
        "hqk,khd->hqd", expo.astype(jnp.bfloat16), value_heads, preferred_element_type=jnp.float32
    )
    attended = (
        (added / new_sum[..., None]).transpose(1, 0, 2).reshape(local_rows, head_count * head_size)
    )
    refined = (
        single_repr.astype(jnp.float32)
        + jnp.dot(
            (gating * attended).astype(jnp.bfloat16), w_out, preferred_element_type=jnp.float32
        )
    ).astype(jnp.bfloat16)
    renormed = norm_rows(refined.astype(jnp.float32)).astype(jnp.bfloat16)
    factor_a = jnp.dot(renormed, w_mix_a, preferred_element_type=jnp.float32).astype(jnp.bfloat16)
    factor_b = jnp.dot(renormed, w_mix_b, preferred_element_type=jnp.float32).astype(jnp.bfloat16)
    every_b = lax.all_gather(factor_b, "rows", axis=0, tiled=True)
    mixed = (
        pair_in + factor_a.astype(jnp.float32)[:, None, :] * every_b.astype(jnp.float32)[None, :, :]
    )
    errors = pair_tail(mixed, w_hidden_a, w_hidden_b, w_hidden_out, w_pae, pae_bias)
    return (refined, errors)


def solution(mesh):
    placed = (
        P("groups", "rows", None),
        P(("groups", "rows"), None),
        P("groups"),
        P("groups"),
        P("groups"),
        P("groups"),
        P(),
        P(),
        P(),
        P(),
        P(),
        P(),
        P(),
        P(),
        P(),
        P(),
        P(),
        P(),
        P(),
        P(),
    )
    return jax.shard_map(
        on_device,
        mesh=mesh,
        in_specs=placed,
        out_specs=(P(("groups", "rows"), None), P(("groups", "rows"), None)),
        check_vma=False,
    )
```

profile of v0, /device:TPU:0, one launch (start us, length us, event | category | flops | bytes accessed | tf_op | source)
XLA Modules:
  0.0 83.6 jit_solution(17553948313955501287)
XLA Ops:
  0.7 7.5 %all-to-all-start = ((bf16[128,8,128]{2,1,0:T(8,128)(2,1)}), bf16[128,8,128]{2,1,0:T(8,128)(2,1)S(1)}, u32[]{:S(2)}, u32[]{:S(2)}) async-start(bf16[128,8,128]{2,1,0:T(8,128)(2,1)} %param.20), calls=%async_computation | async-start | bytes 524288 | tf_op jit(solution)/shard_map/all_to_all | solution.py:78
  8.3 0.8 convert_reduce_fusion
  9.1 0.9 %fusion.30 = f32[8]{0:T(128)S(1)} fusion(bf16[8,384]{1,0:T(8,128)(2,1)} %param.21, f32[8]{0:T(128)S(1)} %broadcast_multiply_fusion.4), kind=kLoop, calls=%fused_computation.57 | loop fusion | flops 12280 | bytes 6208 | tf_op jit(solution)/shard_map/reduce_sum | solution.py:14
  10.0 1.2 %convolution_convert_fusion = bf16[8,384]{1,0:T(8,128)(2,1)S(1)} fusion(bf16[384,384]{1,0:T(8,128)(2,1)} %param.28, bf16[8,384]{1,0:T(8,128)(2,1)} %param.21, f32[8]{0:T(128)S(1)} %add_rsqrt_fusion.3, f32[8]{0:T(128)S(1)} %broadcast_multiply_fusion.4), kind=kOutput, calls=%fused_computation.18 | convolution fusion | flops 2374656 | bytes 307264 | tf_op jit(solution)/shard_map/dot_general | solution.py:76
  11.1 22.1 %all_gather.10 = bf16[128,384]{1,0:T(8,128)(2,1)S(1)} all-gather(bf16[8,384]{1,0:T(8,128)(2,1)S(1)} %convolution_convert_fusion), channel_id=1, replica_groups=mesh['groups'=2,'rows'=16] {'rows'}, dimensions={0}, use_global_device_ids=true | all-gather | bytes 104448 | tf_op jit(solution)/shard_map/all_gather | solution.py:91
  33.4 0.7 dynamic_slice.11
  34.1 0.7 dynamic_slice.10
  34.8 1.2 %convolution_convert_fusion.1 = bf16[8,384]{1,0:T(8,128)(2,1)S(1)} fusion(bf16[384,384]{1,0:T(8,128)(2,1)} %param.27, bf16[8,384]{1,0:T(8,128)(2,1)} %param.21, f32[8]{0:T(128)S(1)} %add_rsqrt_fusion.3, f32[8]{0:T(128)S(1)} %broadcast_multiply_fusion.4), kind=kOutput, calls=%fused_computation.19 | convolution fusion | flops 2374656 | bytes 307264 | tf_op jit(solution)/shard_map/dot_general | solution.py:75
  36.0 1.2 %convolution_convert_fusion.2 = bf16[8,384]{1,0:T(8,128)(2,1)S(1)} fusion(bf16[384,384]{1,0:T(8,128)(2,1)} %param.26, bf16[8,384]{1,0:T(8,128)(2,1)} %param.21, f32[8]{0:T(128)S(1)} %add_rsqrt_fusion.3, f32[8]{0:T(128)S(1)} %broadcast_multiply_fusion.4), kind=kOutput, calls=%fused_computation.20 | convolution fusion | flops 2374656 | bytes 307264 | tf_op jit(solution)/shard_map/dot_general | solution.py:74
  37.2 0.7 broadcast_compare_fusion
  37.9 17.7 %all_gather.9 = bf16[128,384]{1,0:T(8,128)(2,1)S(1)} all-gather(bf16[8,384]{1,0:T(8,128)(2,1)S(1)} %convolution_convert_fusion.1), channel_id=1, replica_groups=mesh['groups'=2,'rows'=16] {'rows'}, dimensions={0}, use_global_device_ids=true | all-gather | bytes 104448 | tf_op jit(solution)/shard_map/all_gather | solution.py:90
  56.1 0.4 fusion.49
  56.6 0.4 multiply_reduce_fusion.2
  57.0 0.5 fusion.13
  57.4 0.2 fusion.50
  57.8 0.2 fusion.2
  58.2 0.5 convert_reduce_fusion.1
  59.1 18.8 %all_gather.11 = bf16[128,128]{1,0:T(8,128)(2,1)S(1)} all-gather(bf16[8,128]{1,0:T(8,128)(2,1)S(1)} %convolution_convert_fusion.3), channel_id=1, replica_groups=mesh['groups'=2,'rows'=16] {'rows'}, dimensions={0}, use_global_device_ids=true | all-gather | bytes 34816 | tf_op jit(solution)/shard_map/all_gather | solution.py:122
  78.3 1.0 %copy.34 = f32[1024,128]{0,1:T(8,128)} copy(f32[1024,128]{1,0:T(8,128)S(1)} %bitcast.47) | data formatting | bytes 1048576 | tf_op jit(solution)/shard_map/reshape | solution.py:29
  79.3 0.4 multiply_reduce_fusion.1
  79.7 0.3 multiply_convert_fusion.2
  80.1 0.4 fusion.55
  80.6 2.0 %fusion.53 = (f32[1024]{0:T(1024)S(1)}, f32[1024,128]{0,1:T(8,128)S(1)}) fusion(f32[1024,128]{0,1:T(8,128)} %copy.34, bf16[512,128]{1,0:T(8,128)(2,1)S(1)} %copy-done.12, f32[1024,512]{1,0:T(8,128)S(1)} %fusion.55, bf16[1024,128]{1,0:T(8,128)(2,1)S(1)} %multiply_convert_fusion.2, bf16[128,512]{1,0:T(8,128)(2,1)S(1)} %copy-done.13), kind=kOutput, calls=%fused_computation.87 | convolution fusion | flops 271842304 | bytes 3674112 | tf_op jit(solution)/shard_map/dot_general | solution.py:34
  82.9 0.7 multiply_reduce_fusion.3
  (63 shorter events, 2.1 us)
Async XLA Ops:
  0.6 57.6 %copy-start = (bf16[384,384]{1,0:T(8,128)(2,1)S(1)}, bf16[384,384]{1,0:T(8,128)(2,1)}, u32[]{:S(2)}) copy-start(bf16[384,384]{1,0:T(8,128)(2,1)} %param.30) | copy-start | bytes 884740
  0.6 55.4 %copy-start.7 = (s32[128]{0:T(128)S(1)}, s32[128]{0:T(128)}, u32[]{:S(2)}) copy-start(s32[128]{0:T(128)} %param.22) | copy-start | bytes 1540
  0.7 55.4 %copy-start.8 = (s32[128]{0:T(128)S(1)}, s32[128]{0:T(128)}, u32[]{:S(2)}) copy-start(s32[128]{0:T(128)} %param.23) | copy-start | bytes 1540
  0.7 55.2 %copy-start.9 = (s32[128]{0:T(128)S(1)}, s32[128]{0:T(128)}, u32[]{:S(2)}) copy-start(s32[128]{0:T(128)} %param.24) | copy-start | bytes 1540
  0.7 55.4 %copy-start.3 = (bf16[66,128]{1,0:T(8,128)(2,1)S(1)}, bf16[66,128]{1,0:T(8,128)(2,1)}, u32[]{:S(2)}) copy-start(bf16[66,128]{1,0:T(8,128)(2,1)} %param.32) | copy-start | bytes 50692
  0.7 56.3 %copy-start.6 = (bf16[128,16]{0,1:T(8,128)(2,1)S(1)}, bf16[128,16]{0,1:T(8,128)(2,1)}, u32[]{:S(2)}) copy-start(bf16[128,16]{0,1:T(8,128)(2,1)} %param.31) | copy-start | bytes 12292
  0.7 55.4 %all-to-all-start = ((bf16[128,8,128]{2,1,0:T(8,128)(2,1)}), bf16[128,8,128]{2,1,0:T(8,128)(2,1)S(1)}, u32[]{:S(2)}, u32[]{:S(2)}) async-start(bf16[128,8,128]{2,1,0:T(8,128)(2,1)} %param.20), calls=%async_computation | async-start | bytes 524288 | tf_op jit(solution)/shard_map/all_to_all | solution.py:78
  11.1 47.1 %copy-start.2 = (bf16[8,384]{1,0:T(8,128)(2,1)S(1)}, bf16[8,384]{1,0:T(8,128)(2,1)}, u32[]{:S(2)}) copy-start(bf16[8,384]{1,0:T(8,128)(2,1)} %param.21) | copy-start | bytes 18436
  11.1 47.1 %copy-start.11 = (bf16[384,384]{1,0:T(8,128)(2,1)S(1)}, bf16[384,384]{1,0:T(8,128)(2,1)}, u32[]{:S(2)}) copy-start(bf16[384,384]{1,0:T(8,128)(2,1)} %param.29) | copy-start | bytes 884740
  36.0 22.9 %copy-start.14 = (bf16[384,128]{1,0:T(8,128)(2,1)S(1)}, bf16[384,128]{1,0:T(8,128)(2,1)}, u32[]{:S(2)}) copy-start(bf16[384,128]{1,0:T(8,128)(2,1)} %param.34) | copy-start | bytes 294916
  37.2 40.7 %copy-start.15 = (bf16[384,128]{1,0:T(8,128)(2,1)S(1)}, bf16[384,128]{1,0:T(8,128)(2,1)}, u32[]{:S(2)}) copy-start(bf16[384,128]{1,0:T(8,128)(2,1)} %param.33) | copy-start | bytes 294916
  58.7 21.8 %copy-start.5 = (bf16[8,384]{1,0:T(8,128)(2,1)}, bf16[8,384]{1,0:T(8,128)(2,1)S(1)}, u32[]{:S(2)}) copy-start(bf16[8,384]{1,0:T(8,128)(2,1)S(1)} %get-tuple-element.11) | copy-start | bytes 18436
  58.7 21.4 %copy-start.1 = (bf16[128,512]{1,0:T(8,128)(2,1)S(1)}, bf16[128,512]{1,0:T(8,128)(2,1)}, u32[]{:S(2)}) copy-start(bf16[128,512]{1,0:T(8,128)(2,1)} %param.36) | copy-start | bytes 393220
  79.3 1.2 %copy-start.12 = (bf16[512,128]{1,0:T(8,128)(2,1)S(1)}, bf16[512,128]{1,0:T(8,128)(2,1)}, u32[]{:S(2)}) copy-start(bf16[512,128]{1,0:T(8,128)(2,1)} %param.37) | copy-start | bytes 393220
  79.3 1.2 %copy-start.13 = (bf16[128,512]{1,0:T(8,128)(2,1)S(1)}, bf16[128,512]{1,0:T(8,128)(2,1)}, u32[]{:S(2)}) copy-start(bf16[128,512]{1,0:T(8,128)(2,1)} %param.35) | copy-start | bytes 393220
  80.5 2.1 %copy-start.4 = (bf16[128,64]{0,1:T(8,128)(2,1)S(1)}, bf16[128,64]{0,1:T(8,128)(2,1)}, u32[]{:S(2)}) copy-start(bf16[128,64]{0,1:T(8,128)(2,1)} %param.38) | copy-start | bytes 49156
  80.6 2.1 %copy-start.10 = (f32[64]{0:T(128)S(1)}, f32[64]{0:T(128)}, u32[]{:S(2)}) copy-start(f32[64]{0:T(128)} %param.39) | copy-start | bytes 772
where the time goes:
time: 84.1 us; the launch traced here: 83.6 us
  blocking collectives  58.6 us (70%)
  matrix products  8.32 us (10%)
  starting transfers between devices  7.53 us (9%)
  other arithmetic  5.09 us (6%)
  local copies, waits for them, and re-layouts  3.06 us (4%)
  between operations  0.98 us (1%)
    all_gather x1, blocking collectives, on_device(): value_part = lax.all_gather(values_local, 'rows', axis=0, tiled=True)  22.1 us
    all_gather x1, blocking collectives, on_device(): every_b = lax.all_gather(factor_b, 'rows', axis=0, tiled=True)  18.8 us
    all_gather x1, blocking collectives, on_device(): key_part = lax.all_gather(keys_local, 'rows', axis=0, tiled=True)  17.7 us
    all_to_all x1, starting transfers between devices, on_device(): lax.all_to_all(pair_repr, 'rows', split_axis=0, concat_axis=1, tiled=True)  7.53 us
    dot_general x1, matrix products, pair_tail(): jnp.dot(hidden, w_hidden_out, preferred_element_type=jnp.float32)  1.96 us
    reduce_sum x5, other arithmetic, norm_rows(): spread = jnp.mean(center * center, axis=-1, keepdims=True)  1.87 us
  transfers between devices with their start and end apart: 1, of which 0 were waited for; matrix products, arithmetic and copies ran while one was open for 10% of the time, Pallas kernels for 0%

commit v1 on v0

v1 whole, which is shorter than its diff:
```python
import functools
import math

import jax
import jax.numpy as jnp
from jax import lax
from jax.experimental import pallas as pl
from jax.experimental.pallas import tpu as pltpu
from jax.sharding import PartitionSpec as P

epsilon = 1e-05
masked_score = -1e30
chain_step = 65536.0
f32 = jnp.float32
bf16 = jnp.bfloat16


def norm_rows(values):
    center = values - jnp.mean(values, axis=-1, keepdims=True)
    spread = jnp.mean(center * center, axis=-1, keepdims=True)
    return center * lax.rsqrt(spread + epsilon)


def mm(a, b):
    return jnp.dot(a, b, preferred_element_type=f32)


def mm_nt(a, b):
    return lax.dot_general(a, b, (((1,), (1,)), ((), ())), preferred_element_type=f32)


def column(row):
    m = row.shape[1]
    pick = lax.broadcasted_iota(jnp.int32, (m, m), 0) == lax.broadcasted_iota(jnp.int32, (m, m), 1)
    return jnp.sum(jnp.where(pick, row, 0.0), axis=1, keepdims=True)


def bucket_onehot(diff, classes):
    reach = (classes - 2) // 2
    same = jnp.abs(diff) < 0.5 * chain_step
    bucket = jnp.where(same, jnp.clip(diff, -reach, reach) + reach, 2.0 * reach + 1.0)
    lanes = lax.broadcasted_iota(jnp.int32, bucket.shape, bucket.ndim - 1).astype(f32)
    return jnp.where(bucket == lanes, 1.0, 0.0).astype(bf16)


def kernel(
    n,
    heads,
    pair_h, single_h, res_h, chain_h, complex_h, pad_h,
    wq_h, wk_h, wv_h, wg_h, wo_h, wb_h, rel_h, wma_h, wmb_h, wha_h, whb_h, who_h, wp_h, pb_h,
    refined_ref, errors_ref,
    pair_v, single_v, res_v, chain_v, complex_v, pad_v,
    wq_v, wk_v, wv_v, wg_v, wo_v, wb_v, rel_v, wma_v, wmb_v, wha_v, whb_v, who_v, wp_v, pb_v,
    code_v, ccol_v, bias_s, bias_r, single_r, pair_r, b_s, b_r, a_v, pin_v, score_v,
    local_sem, own_sem, send_sem, recv_sem,
):
    me = lax.axis_index("rows")
    count, rows, width = pair_h.shape
    classes = rel_h.shape[0]
    inner = single_h.shape[1]
    head_size = inner // heads
    first = pl.multiple_of(me * rows, rows)

    hbm = (pair_h, single_h, res_h, chain_h, complex_h, pad_h, wq_h, wk_h, wv_h, wg_h, wo_h,
           wb_h, rel_h, wma_h, wmb_h, wha_h, whb_h, who_h, wp_h, pb_h)
    vmem = (pair_v, single_v, res_v, chain_v, complex_v, pad_v, wq_v, wk_v, wv_v, wg_v, wo_v,
            wb_v, rel_v, wma_v, wmb_v, wha_v, whb_v, who_v, wp_v, pb_v)
    (PAIR, SINGLE, RES, CHAIN, COMPLEX, PAD, WQ, WK, WV, WG, WO, WB, REL, WMA, WMB, WHA, WHB,
     WHO, WP, PB) = range(len(hbm))
    loads = [pltpu.make_async_copy(h, v, local_sem.at[i]) for i, (h, v) in enumerate(zip(hbm, vmem))]

    barrier = pltpu.get_barrier_semaphore()

    def greet(s, _):
        pl.semaphore_signal(
            barrier, inc=1, device_id={"rows": lax.rem(me + s, n)},
            device_id_type=pl.DeviceIdType.MESH,
        )
        return 0

    lax.fori_loop(1, n, greet, 0)
    for i in (RES, CHAIN, REL, WB, PAIR, SINGLE, COMPLEX, PAD, WQ, WG, WK, WV, WO, WMB, WMA,
              WHA, WHB, WHO, WP, PB):
        loads[i].start()

    for i in (RES, CHAIN, COMPLEX):
        loads[i].wait()
    step = min(count, 128)
    for k in range(0, count, step):
        code = chain_v[:, k:k + step].astype(f32) * chain_step + res_v[:, k:k + step].astype(f32)
        code_v[k:k + step, :] = jnp.broadcast_to(column(code), (step, 128))
        ccol_v[k:k + step, :] = jnp.broadcast_to(
            column(complex_v[:, k:k + step].astype(f32)), (step, 128))

    for i in (REL, WB, PAIR):
        loads[i].wait()
    rel = rel_v[...]
    spots = rows * heads
    tile_h = jnp.where(
        lax.broadcasted_iota(jnp.int32, (heads, spots), 1) % heads
        == lax.broadcasted_iota(jnp.int32, (heads, spots), 0), 1.0, 0.0).astype(bf16)
    w_tiled = lax.dot_general(
        wb_v[...], tile_h, (((0,), (0,)), ((), ())), preferred_element_type=f32).astype(bf16)
    code_keys = code_v[pl.ds(first, rows), :classes]

    def bias_block(j, _):
        at = pl.multiple_of(j * step, step)
        code_i = code_v[pl.ds(at, step), :classes]
        diff = code_i[:, None, :] - code_keys[None, :, :]
        hot = bucket_onehot(diff.reshape(step * rows, classes), classes)
        cells = mm(hot, rel) + pair_v[pl.ds(at, step)].astype(f32).reshape(step * rows, width)
        out = mm(norm_rows(cells).astype(bf16), w_tiled)
        out = out.reshape(step // rows, rows, rows, spots)
        lane_q = lax.broadcasted_iota(jnp.int32, (1, 1, spots), 2) // heads
        total = jnp.where(lane_q == 0, out[:, 0], 0.0)
        for q in range(1, rows):
            total = jnp.where(lane_q == q, out[:, q], total)
        bias_s[pl.ds(pl.multiple_of(j * (step // rows), step // rows), step // rows)] = total.astype(bf16)
        return 0

    lax.fori_loop(0, count // step, bias_block, 0, unroll=count == step)
    loads[SINGLE].wait()

    pl.semaphore_wait(barrier, n - 1)

    def remote(src, dst, i, peer):
        return pltpu.make_async_remote_copy(
            src_ref=src, dst_ref=dst, send_sem=send_sem.at[i], recv_sem=recv_sem.at[i],
            device_id={"rows": peer}, device_id_type=pl.DeviceIdType.MESH)

    def send_single(s, _):
        peer = lax.rem(me + s, n)
        remote(single_v, single_r.at[me], 0, peer).start()
        return 0

    def send_bias(s, _):
        peer = lax.rem(me + s, n)
        remote(bias_s.at[peer], bias_r.at[me], 1, peer).start()
        return 0

    def send_pair(s, _):
        peer = lax.rem(me + s, n)
        remote(pair_v.at[pl.ds(peer * rows, rows)], pair_r.at[:, me], 2, peer).start()
        return 0

    lax.fori_loop(1, n, send_single, 0)
    lax.fori_loop(1, n, send_bias, 0)
    lax.fori_loop(1, n, send_pair, 0)
    own = (
        pltpu.make_async_copy(single_v, single_r.at[me], own_sem.at[0]),
        pltpu.make_async_copy(bias_s.at[me], bias_r.at[me], own_sem.at[1]),
        pltpu.make_async_copy(pair_v.at[pl.ds(first, rows)], pair_r.at[:, me], own_sem.at[2]),
    )
    for copy in own:
        copy.start()

    mine = single_v[...].astype(f32)
    normed = norm_rows(mine).astype(bf16)
    loads[WQ].wait()
    queries = mm(normed, wq_v[...]).astype(bf16).astype(f32)
    loads[WG].wait()
    gating = jax.nn.sigmoid(mm(normed, wg_v[...]))
    head_of = lax.broadcasted_iota(jnp.int32, (heads, inner), 1) // head_size
    own_head = head_of == lax.broadcasted_iota(jnp.int32, (heads, inner), 0)
    q_wide = jnp.concatenate(
        [jnp.where(own_head, queries[q:q + 1, :], 0.0) for q in range(rows)], axis=0).astype(bf16)

    def rel_block(q, _):
        diff = code_v[pl.ds(first + q, 1), :classes] - code_v[:, :classes]
        pin_v[q] = mm(bucket_onehot(diff, classes), rel)
        return 0

    lax.fori_loop(0, rows, rel_block, 0, unroll=count == step)

    loads[WK].wait()
    loads[WV].wait()
    own[0].wait()
    landed = single_r.at[pl.ds(0, n - 1)]
    pltpu.make_async_copy(landed, landed, recv_sem.at[0]).wait()
    every = norm_rows(single_r[...].astype(f32).reshape(count, inner)).astype(bf16)
    keys = mm(every, wk_v[...]).astype(bf16)
    values = mm(every, wv_v[...]).astype(bf16)
    scores = mm_nt(q_wide, keys) / math.sqrt(head_size)
    loads[PAD].wait()
    key_ids = lax.broadcasted_iota(jnp.int32, (1, count), 1)
    complex_row = complex_v[...].astype(f32)
    real = pad_v[...] == 1
    own[1].wait()
    landed = bias_r.at[pl.ds(0, n - 1)]
    pltpu.make_async_copy(landed, landed, recv_sem.at[1]).wait()
    eye = jnp.where(
        lax.broadcasted_iota(jnp.int32, (spots, spots), 0)
        == lax.broadcasted_iota(jnp.int32, (spots, spots), 1), 1.0, 0.0).astype(bf16)
    arrived = bias_r[...].astype(f32).reshape(count, spots).astype(bf16)
    scores = scores + mm_nt(eye, arrived)
    for q in range(rows):
        allowed = (ccol_v[pl.ds(first + q, 1), 0:1] == complex_row) & (real | (key_ids == first + q))
        part = scores[q * heads:(q + 1) * heads, :]
        score_v[q * heads:(q + 1) * heads, :] = jnp.where(allowed, part, masked_score)
    scores = score_v[...]
    expo = jnp.exp(scores - jnp.max(scores, axis=-1, keepdims=True))
    total = jnp.sum(expo, axis=-1, keepdims=True)
    mixed_heads = mm(expo.astype(bf16), values) / total
    attended = jnp.concatenate(
        [jnp.sum(jnp.where(own_head, mixed_heads[q * heads:(q + 1) * heads, :], 0.0),
                 axis=0, keepdims=True) for q in range(rows)], axis=0)
    loads[WO].wait()
    refined = (mine + mm((gating * attended).astype(bf16), wo_v[...])).astype(bf16)
    renormed = norm_rows(refined.astype(f32)).astype(bf16)
    loads[WMB].wait()
    b_s[...] = mm(renormed, wmb_v[...]).astype(bf16)
    b_r[me] = b_s[...]
    loads[WMA].wait()
    a_v[...] = mm(renormed, wma_v[...]).astype(bf16).astype(f32)

    def send_b(s, _):
        remote(b_s, b_r.at[me], 3, lax.rem(me + s, n)).start()
        return 0

    lax.fori_loop(1, n, send_b, 0)
    refined_ref[...] = refined

    own[2].wait()
    landed = pair_r.at[:, pl.ds(0, n - 1)]
    pltpu.make_async_copy(landed, landed, recv_sem.at[2]).wait()

    def add_block(q, _):
        pin_v[q] = pin_v[q] + pair_r[q].astype(f32).reshape(count, width)
        return 0

    lax.fori_loop(0, rows, add_block, 0, unroll=count == step)
    for i in (WHA, WHB, WHO, WP, PB):
        loads[i].wait()
    bins = wp_v.shape[0]
    bias_col = column(pb_v[...])
    centers = (lax.broadcasted_iota(jnp.int32, (bins, 1), 0).astype(f32) + 0.5) * (32.0 / bins)
    landed = b_r.at[pl.ds(0, n - 1)]
    pltpu.make_async_copy(landed, landed, recv_sem.at[3]).wait()

    def tail(c, _):
        at = pl.multiple_of(c * step, step)
        tile = pl.multiple_of(c * (step // rows), step // rows)
        factor_b = b_r[pl.ds(tile, step // rows)].astype(f32).reshape(step, width)
        found = []
        for q in range(rows):
            flat = pin_v[q, pl.ds(at, step), :] + a_v[q:q + 1, :] * factor_b
            x = norm_rows(flat).astype(bf16)
            gate = mm(x, wha_v[...])
            up = mm(x, whb_v[...])
            half = 0.5 * gate
            hidden = ((half + half * jnp.tanh(half)) * up).astype(bf16)
            updated = flat + mm(hidden, who_v[...])
            final = norm_rows(updated).astype(bf16)
            logits = mm_nt(wp_v[...], final) + bias_col
            expo = jnp.exp(logits - jnp.max(logits, axis=0, keepdims=True))
            found.append(jnp.sum(expo * centers, axis=0, keepdims=True)
                         / jnp.sum(expo, axis=0, keepdims=True))
        errors_ref[:, pl.ds(at, step)] = jnp.concatenate(found, axis=0)
        return 0

    lax.fori_loop(0, count // step, tail, 0, unroll=count == step)

    for i, buf in enumerate((single_r, bias_r, None, b_r)):
        sent = pair_r.at[:, pl.ds(0, n - 1)] if buf is None else buf.at[pl.ds(0, n - 1)]
        pltpu.make_async_copy(sent, sent, send_sem.at[i]).wait()


def on_device(n, pair_repr, single_repr, residue_index, chain_index, complex_index, pad_mask,
              w_query, w_key, w_value, w_gate, w_out, w_bias, rel_table, w_mix_a, w_mix_b,
              w_hidden_a, w_hidden_b, w_hidden_out, w_pae, pae_bias):
    count, rows, width = pair_repr.shape
    inner = single_repr.shape[1]
    heads = w_bias.shape[1]
    args = (pair_repr, single_repr, residue_index[None], chain_index[None], complex_index[None],
            pad_mask[None], w_query, w_key, w_value, w_gate, w_out, w_bias.T, rel_table,
            w_mix_a, w_mix_b, w_hidden_a, w_hidden_b, w_hidden_out, w_pae.T, pae_bias[None])
    spots = rows * heads
    scratch = [pltpu.VMEM(a.shape, a.dtype) for a in args] + [
        pltpu.VMEM((count, 128), f32),
        pltpu.VMEM((count, 128), f32),
        pltpu.VMEM((n, rows, spots), bf16),
        pltpu.VMEM((n, rows, spots), bf16),
        pltpu.VMEM((n, rows, inner), bf16),
        pltpu.VMEM((rows, n, rows, width), bf16),
        pltpu.VMEM((rows, width), bf16),
        pltpu.VMEM((n, rows, width), bf16),
        pltpu.VMEM((rows, width), f32),
        pltpu.VMEM((rows, count, width), f32),
        pltpu.VMEM((spots, count), f32),
        pltpu.SemaphoreType.DMA((len(args),)),
        pltpu.SemaphoreType.DMA((3,)),
        pltpu.SemaphoreType.DMA((4,)),
        pltpu.SemaphoreType.DMA((4,)),
    ]
    return pl.pallas_call(
        functools.partial(kernel, n, heads),
        out_shape=(
            jax.ShapeDtypeStruct((rows, inner), bf16),
            jax.ShapeDtypeStruct((rows, count), f32),
        ),
        in_specs=[pl.BlockSpec(memory_space=pltpu.HBM)] * len(args),
        out_specs=[pl.BlockSpec(memory_space=pltpu.VMEM)] * 2,
        scratch_shapes=scratch,
        compiler_params=pltpu.CompilerParams(
            collective_id=0, has_side_effects=True, vmem_limit_bytes=60 * 1024 * 1024),
        name="confidence",
    )(*args)


def solution(mesh):
    placed = (
        P("groups", "rows", None),
        P(("groups", "rows"), None),
        P("groups"),
        P("groups"),
        P("groups"),
        P("groups"),
    ) + (P(),) * 14
    return jax.shard_map(
        functools.partial(on_device, mesh.shape["rows"]),
        mesh=mesh,
        in_specs=placed,
        out_specs=(P(("groups", "rows"), None), P(("groups", "rows"), None)),
        check_vma=False,
    )
```

time: 84.1 us -> 26 us (0.31)
  blocking collectives: 58.6 us -> 0 us
  Pallas kernels: 0 us -> 23.3 us
  matrix products: 8.32 us -> 0 us
  starting transfers between devices: 7.53 us -> 0 us
  other arithmetic: 5.09 us -> 0 us
  local copies, waits for them, and re-layouts: 3.06 us -> 1.88 us
    all_gather x3 -> x0, blocking collectives: 58.6 us -> none  [the longest x1 22.1 us: on_device(): value_part = lax.all_gather(values_local, 'rows', axis=0, tiled=True)]
    pallas_call x0 -> x1, Pallas kernels: none -> 23.3 us  [on_device(): pl.pallas_call(functools.partial(kernel, n, heads), out_shape=(jax.ShapeD...]
    dot_general x13 -> x0, matrix products: 8.32 us -> none  [the longest x1 1.96 us: pair_tail(): jnp.dot(hidden, w_hidden_out, preferred_element_type=jnp.float32)]
    all_to_all x1 -> x0, starting transfers between devices: 7.53 us -> none  [on_device(): lax.all_to_all(pair_repr, 'rows', split_axis=0, concat_axis=1, tiled=True)]
    reduce_sum x10 -> x0, other arithmetic: 3.81 us -> none  [the longest x5 1.87 us: norm_rows(): spread = jnp.mean(center * center, axis=-1, keepdims=True)]
    unnamed x32 -> x4, local copies, waits for them, and re-layouts: 0.08 us -> 1.88 us
    dynamic_slice x3 -> x0, local copies, waits for them, and re-layouts: 1.54 us -> none  [the longest x1 0.73 us: on_device(): lax.dynamic_slice_in_dim(residue_index, first_row, local_rows, 0)]
    reshape x3 -> x0, local copies, waits for them, and re-layouts: 1.18 us -> none  [the longest x1 0.99 us: pair_tail(): flat = mixed.reshape(-1, width)]
  transfers between devices with their start and end apart: 1 -> 0, of which waited for: 0 -> 0; matrix products, arithmetic and copies ran while one was open for 10% -> 0% of each run, Pallas kernels for 0% -> 0%
where the time goes in v1:
time: 26 us; the launch traced here: 25.8 us
  Pallas kernels  23.3 us (90%)
  local copies, waits for them, and re-layouts  1.88 us (7%)
  between operations  0.66 us (3%)
    pallas_call x1, Pallas kernels, on_device(): pl.pallas_call(functools.partial(kernel, n, heads), out_shape=(jax.ShapeD...  23.3 us
    unnamed x4, local copies, waits for them, and re-layouts  1.88 us

profile of v1, /device:TPU:0, one launch (start us, length us, event | category | flops | bytes accessed | tf_op | source)
XLA Modules:
  0.0 25.8 jit_solution(6184261201672486467)
XLA Ops:
  0.6 23.3 %confidence.1 = (bf16[8,384]{1,0:T(8,128)(2,1)}, f32[8,128]{1,0:T(8,128)}) custom-call(bf16[128,8,128]{2,1,0:T(8,128)(2,1)} %pair_h.1, bf16[8,384]{1,0:T(8,128)(2,1)} %single_h.1, s32[1,128]{1,0:T(1,128)} %bitcast.9, s32[1,128]{1,0:T(1,128)} %bitcast.10, s32[1,128]{1,0:T(1,128)} %bitcast.11, s32[1,128]{1,0:T(1,128)} %bitcast.12, bf16[384,384]{1,0:T(8,128)(2,1)} %wq_h.1, ...), custom_call_target="tpu_custom_call" | custom-call | tf_op jit(solution)/shard_map/confidence/pallas_call | solution.py:295
  23.9 0.0 copy-start
  23.9 1.3 %copy.24 = bf16[8,384]{1,0:T(8,128)(2,1)} copy(bf16[8,384]{1,0:T(8,128)(2,1)} %get-tuple-element.4) | data formatting | bytes 12288
  25.2 0.0 copy-done
  25.2 0.6 %copy.25 = f32[8,128]{1,0:T(8,128)} copy(f32[8,128]{1,0:T(8,128)S(1)} %copy-done) | data formatting | bytes 8192
Async XLA Ops:
  23.9 1.3 %copy-start = (f32[8,128]{1,0:T(8,128)S(1)}, f32[8,128]{1,0:T(8,128)}, u32[]{:S(2)}) copy-start(f32[8,128]{1,0:T(8,128)} %get-tuple-element.5) | copy-start | bytes 12292
